TPU v7x, 32 devices: a whole 2x2x4 slice. The times are simulated.
32 devices in a mesh: row: 8 (over y, x, core), col: 4 (over z).
Axes of the slice: x: 2, y: 2, z: 4, core: 2. Of those that a mesh axis runs over, the one named last changes fastest.
Arguments:
- velocity: float32 [128, 128, 2048], P(None, 'row', 'col'), may hold values from -6 to 6
- symbol_x: float32 [128], replicated, may hold values from 0.3 to 3
- symbol_y: float32 [128], replicated, may hold values from 0.3 to 3
- symbol_z: float32 [2048], replicated, may hold values from 0.3 to 3
Outputs:
- coefficients: float32 [128, 128, 2048], P('row', 'col')
All inputs are finite; a program needn't handle non-finite values.
Results may differ from a plain program's by a relative error of at most 0.000076.
Values sent between devices are 32-bit elements; how exact they have to be, the bound alone decides.
A program may use at most 192 MiB of HBM per device.

v0:
```python
import functools

import jax
import jax.numpy as jnp
import numpy as np
from jax import lax
from jax.experimental import pallas as pl
from jax.experimental.pallas import tpu as pltpu
from jax.sharding import PartitionSpec as P

SUB = 8
MESH = pl.DeviceIdType.MESH


def mode_table(count):
    rank = jnp.arange(count)
    angle = 2.0 * jnp.pi / count * (rank[:, None] * rank[None, :] % count).astype(jnp.float32)
    return (jnp.cos(angle) + jnp.sin(angle)) * count ** (-0.5)


def along_dim(values, dim):
    moved = jnp.tensordot(
        values, mode_table(values.shape[dim]), axes=([dim], [0]), precision=lax.Precision.HIGHEST
    )
    return jnp.moveaxis(moved, -1, dim)


def fixed_table(count):
    rank = np.arange(count)
    angle = 2.0 * np.pi / count * (rank[:, None] * rank[None, :] % count)
    return ((np.cos(angle) + np.sin(angle)) * count ** (-0.5)).astype(np.float32)


def halves(table):
    high = table.astype(jnp.bfloat16)
    low = (table - high.astype(np.float32)).astype(jnp.bfloat16)
    return high, low


def split(values):
    high = values.astype(jnp.bfloat16)
    low = (values - high.astype(jnp.float32)).astype(jnp.bfloat16)
    return high, low


def product(a, b):
    return jnp.dot(a, b, preferred_element_type=jnp.float32)


def flipped(index, mask):
    out = index
    bit = 1
    while bit <= mask:
        if mask & bit:
            out = out + bit * (1 - 2 * ((index // bit) % 2))
        bit *= 2
    return out


def kernel(
    dims, v_hbm, w_hbm, t_hbm, sx_ref, sy_ref, sz_ref, out_ref,
    v, w, t, v_parts, xs, rbuf, ybuf, zbuf, lhs, sx_col, sy_col,
    load_sem, row_send, row_recv, col_send, col_recv,
):
    rows, cols, chunks, per, ahead, lag = dims
    part_y, part_z = v.shape[1], v.shape[2]
    grid_x, grid_y = v.shape[0], rbuf.shape[1]
    share_y, grid_z = zbuf.shape[1], zbuf.shape[2]
    tiles, tile = t.shape[1], t.shape[3]
    r, c = lax.axis_index("row"), lax.axis_index("col")

    pieces = 4 if grid_x % (4 * SUB) == 0 else 1
    piece = grid_x // pieces
    load_v = [
        pltpu.make_async_copy(
            v_hbm.at[pl.ds(p * piece, piece)], v.at[pl.ds(p * piece, piece)], load_sem.at[3 + p]
        )
        for p in range(pieces)
    ]
    load_w = pltpu.make_async_copy(w_hbm.at[0], w.at[0], load_sem.at[1])
    load_rest = pltpu.make_async_copy(w_hbm.at[pl.ds(1, chunks - 1)], w.at[pl.ds(1, chunks - 1)], load_sem.at[2])
    load_t = pltpu.make_async_copy(t_hbm, t, load_sem.at[0])
    for load in load_v:
        load.start()
    load_w.start()

    row_masks = sorted(range(1, rows), key=lambda m: (-bin(m // 2).count("1"), m))
    row_peers = [flipped(r, m) for m in row_masks]
    col_peers = [flipped(c, m) for m in range(1, cols)]

    barrier = pltpu.get_barrier_semaphore()
    for s in row_peers:
        pl.semaphore_signal(barrier, inc=1, device_id=(s, c), device_id_type=MESH)
    for s in col_peers:
        pl.semaphore_signal(barrier, inc=1, device_id=(r, s), device_id_type=MESH)

    for ref, column in ((sx_ref, sx_col), (sy_ref, sy_col)):
        column[...] = jnp.broadcast_to(ref[...], (128, ref.shape[1])).T
    step = SUB * SUB

    def part_loop(i, carry):
        for g in range(part_y // SUB):
            block = v[pl.ds(i * SUB, SUB), g * SUB:(g + 1) * SUB, :].reshape(step, part_z)
            high, low = split(block)
            v_parts[g, 0, pl.ds(pl.multiple_of(i * step, step), step), :] = high
            v_parts[g, 1, pl.ds(pl.multiple_of(i * step, step), step), :] = low
        return carry

    for p in range(pieces):
        load_v[p].wait()
        lax.fori_loop(p * piece // SUB, (p + 1) * piece // SUB, part_loop, 0)
    load_w.wait()
    load_rest.start()
    load_t.start()
    pl.semaphore_wait(barrier, len(row_peers) + len(col_peers))

    def x_stage(k):
        m, depth = rows * per * SUB, grid_x * SUB
        for g in range(part_y // SUB):
            both = product(w[k, :2 * m, :depth], v_parts[g, 0])
            sums = both[:m] + both[m:] + product(w[k, :m, :depth], v_parts[g, 1])
            xs[k, :, g * SUB:(g + 1) * SUB, :] = sums.reshape(rows * per, SUB, part_z)

    def own_rows():
        return pl.ds(pl.multiple_of(r * part_y, SUB), part_y)

    def row_stage(k):
        for i in range(per):
            for s in row_peers:
                pltpu.make_async_remote_copy(
                    src_ref=xs.at[k, s * per + i],
                    dst_ref=rbuf.at[k * per + i, own_rows(), :],
                    send_sem=row_send.at[k], recv_sem=row_recv.at[k, i],
                    device_id=(s, c), device_id_type=MESH,
                ).start()
        rbuf[pl.ds(k * per, per), own_rows(), :] = xs[k, pl.ds(r * per, per)]

    def y_stage(k):
        for i in range(per):
            came = rbuf.at[k * per + i, pl.ds(0, grid_y - part_y), :]
            pltpu.make_async_copy(came, came, row_recv.at[k, i]).wait()
            high, low = split(rbuf[k * per + i])
            both = product(w[0, :2 * grid_y, grid_x * SUB:], high)
            ybuf[k, i] = both[:grid_y] + both[grid_y:] + product(w[0, :grid_y, grid_x * SUB:], low)
            for m, s in enumerate(col_peers):
                pltpu.make_async_remote_copy(
                    src_ref=ybuf.at[k, i, pl.ds(pl.multiple_of(s * share_y, SUB), share_y), :],
                    dst_ref=zbuf.at[k * per + i, :, pl.ds(pl.multiple_of(c * part_z, 128), part_z)],
                    send_sem=col_send.at[k], recv_sem=col_recv.at[k, m],
                    device_id=(r, s), device_id_type=MESH,
                ).start()
        zbuf[pl.ds(k * per, per), :, pl.ds(pl.multiple_of(c * part_z, 128), part_z)] = (
            ybuf[k, :, pl.ds(pl.multiple_of(c * share_y, SUB), share_y), :]
        )

    def col_wait(k, m):
        came = zbuf.at[pl.ds(k * per, per), :, pl.ds(0, part_z)]
        pltpu.make_async_copy(came, came, col_recv.at[k, m]).wait()

    def scaled(k, n, sums):
        y_part = sy_col[pl.ds(pl.multiple_of(c * share_y, SUB), share_y), :]
        z_part = sz_ref[:, pl.ds(pl.multiple_of(n * tile, tile), tile)]
        plane = jnp.concatenate([y_part] * (tile // 128), axis=1) + z_part
        for i in range(per):
            x_part = sx_col[pl.ds(r * chunks * per + k * per + i, 1), :]
            symbol = jnp.concatenate([x_part] * (tile // 128), axis=1) + plane
            factor = (1.0 - 0.2 * symbol) / (1.0 + 0.2 * symbol)
            out_ref[k * per + i, :, pl.ds(pl.multiple_of(n * tile, tile), tile)] = (
                sums[i * share_y:(i + 1) * share_y] * factor
            )

    size = per * share_y

    def z_stage(k):
        for m in range(len(col_peers)):
            col_wait(k, m)
        high, low = split(zbuf[pl.ds(k * per, per)].reshape(size, grid_z))
        lhs[:size] = high
        lhs[size:] = low

        def tile_loop(n, carry):
            both = product(lhs[...], t[0, n])
            scaled(k, n, both[:size] + both[size:] + product(lhs[:size], t[1, n]))
            return carry

        lax.fori_loop(0, tiles, tile_loop, 0)

    def last_z_stage(k):
        for m, s in enumerate([c] + col_peers):
            if m > 0:
                col_wait(k, m - 1)
            span = pl.ds(pl.multiple_of(s * part_z, 128), part_z)
            high, low = split(zbuf[pl.ds(k * per, per), :, span].reshape(size, part_z))
            lhs[:size, :part_z] = high
            lhs[size:, :part_z] = low

            def tile_loop(n, carry):
                both = product(lhs[:, :part_z], t[0, n, span, :])
                sums = both[:size] + both[size:] + product(lhs[:size, :part_z], t[1, n, span, :])
                at = pl.ds(pl.multiple_of(n * tile, tile), tile)
                if m > 0:
                    sums = sums + out_ref[pl.ds(k * per, per), :, at].reshape(size, tile)
                if m < len(col_peers):
                    out_ref[pl.ds(k * per, per), :, at] = sums.reshape(per, share_y, tile)
                else:
                    scaled(k, n, sums)
                return carry

            lax.fori_loop(0, tiles, tile_loop, 0)

    def loop(k, carry):
        @pl.when(k == 1)
        def _():
            load_rest.wait()

        @pl.when(k < chunks)
        def _():
            x_stage(k)
            row_stage(k)

        @pl.when((k >= ahead) & (k < chunks + ahead))
        def _():
            y_stage(k - ahead)

        @pl.when(k == ahead + lag)
        def _():
            load_t.wait()

        @pl.when(k >= ahead + lag)
        def _():
            z_stage(k - ahead - lag)

        return carry

    lax.fori_loop(0, chunks + ahead + lag - 1, loop, 0)
    last_z_stage(chunks - 1)

    def drain(k, carry):
        sent = rbuf.at[pl.ds(k * per, per), pl.ds(0, grid_y - part_y), :]
        pltpu.make_async_copy(sent, sent, row_send.at[k]).wait()
        sent = zbuf.at[pl.ds(k * per, per), :, pl.ds(0, grid_z - part_z)]
        pltpu.make_async_copy(sent, sent, col_send.at[k]).wait()
        return carry

    lax.fori_loop(0, chunks, drain, 0)


def transformed(rows, cols, velocity, symbol_x, symbol_y, symbol_z):
    grid_x, part_y, part_z = velocity.shape
    grid_y, grid_z = part_y * rows, part_z * cols
    share_x, share_y = grid_x // rows, grid_y // cols
    chunks = min(8, share_x)
    per = share_x // chunks
    tile = 256
    hx, hy, hz = fixed_table(grid_x), fixed_table(grid_y), fixed_table(grid_z)
    order = np.arange(grid_x).reshape(rows, chunks, per).transpose(1, 0, 2).reshape(chunks, rows * per)
    w = np.stack([np.kron(hx[o], np.eye(SUB, dtype=np.float32)) for o in order])
    w = np.concatenate(halves(w), axis=1)
    h = np.concatenate(halves(hy), axis=0)
    t = np.stack(halves(hz)).reshape(2, grid_z, grid_z // tile, tile).transpose(0, 2, 1, 3)
    held = np.zeros((chunks, max(w.shape[1], h.shape[0]), w.shape[2] + h.shape[1]), w.dtype)
    held[:, :w.shape[1], :w.shape[2]] = w
    held[0, :h.shape[0], w.shape[2]:] = h
    f32, bf16 = jnp.float32, jnp.bfloat16
    hbm = pl.BlockSpec(memory_space=pltpu.HBM)
    vmem = pl.BlockSpec(memory_space=pltpu.VMEM)
    return pl.pallas_call(
        functools.partial(kernel, (rows, cols, chunks, per, 1, 2)),
        out_shape=jax.ShapeDtypeStruct((share_x, share_y, grid_z), f32),
        in_specs=[hbm, hbm, hbm, vmem, vmem, vmem],
        out_specs=vmem,
        scratch_shapes=[
            pltpu.VMEM(velocity.shape, f32),
            pltpu.VMEM(held.shape, bf16),
            pltpu.VMEM(t.shape, bf16),
            pltpu.VMEM((part_y // SUB, 2, grid_x * SUB, part_z), bf16),
            pltpu.VMEM((chunks, rows * per, part_y, part_z), f32),
            pltpu.VMEM((share_x, grid_y, part_z), f32),
            pltpu.VMEM((chunks, per, grid_y, part_z), f32),
            pltpu.VMEM((share_x, share_y, grid_z), f32),
            pltpu.VMEM((2 * per * share_y, grid_z), bf16),
            pltpu.VMEM((grid_x, 128), f32),
            pltpu.VMEM((grid_y, 128), f32),
            pltpu.SemaphoreType.DMA((7,)),
            pltpu.SemaphoreType.DMA((chunks,)),
            pltpu.SemaphoreType.DMA((chunks, per)),
            pltpu.SemaphoreType.DMA((chunks,)),
            pltpu.SemaphoreType.DMA((chunks, cols - 1)),
        ],
        compiler_params=pltpu.CompilerParams(
            collective_id=0, has_side_effects=True, vmem_limit_bytes=46 * 2**20
        ),
    )(velocity, jnp.asarray(held), jnp.asarray(np.ascontiguousarray(t)),
      symbol_x[None, :], symbol_y[None, :], symbol_z[None, :])


def fits(rows, cols, shape):
    grid_x, part_y, part_z = shape
    grid_z = part_z * cols
    held = 7 * grid_x * part_y * part_z * 4 + 4 * grid_z * grid_z + 4 * (grid_x * SUB) ** 2
    even = rows & (rows - 1) == 0 and cols & (cols - 1) == 0 and grid_x % (8 * rows) == 0
    return even and part_y % SUB == 0 and part_z % 128 == 0 and (part_y * rows) % (SUB * cols) == 0 and held < 54 * 2**20


def local(rows, cols, velocity, symbol_x, symbol_y, symbol_z):
    if fits(rows, cols, velocity.shape):
        return transformed(rows, cols, velocity, symbol_x, symbol_y, symbol_z)
    part_values = along_dim(velocity, 0)
    part_values = lax.all_to_all(part_values, "row", split_axis=0, concat_axis=1, tiled=True)
    pencil_values = along_dim(part_values, 1)
    pencil_values = lax.all_to_all(pencil_values, "col", split_axis=1, concat_axis=2, tiled=True)
    pencil_values = along_dim(pencil_values, 2)
    share_x = pencil_values.shape[0]
    part_x = lax.dynamic_slice_in_dim(symbol_x, lax.axis_index("row") * share_x, share_x)
    share_y = pencil_values.shape[1]
    part_y = lax.dynamic_slice_in_dim(symbol_y, lax.axis_index("col") * share_y, share_y)
    symbol = part_x[:, None, None] + part_y[None, :, None] + symbol_z[None, None, :]
    return pencil_values * ((1.0 - 0.2 * symbol) / (1.0 + 0.2 * symbol))


def solution(mesh):
    placed = (P(None, "row", "col"), P(), P(), P())
    return jax.shard_map(
        functools.partial(local, mesh.shape["row"], mesh.shape["col"]),
        mesh=mesh, in_specs=placed, out_specs=P("row", "col", None), check_vma=False,
    )
```

profile of v0, /device:TPU:0, one launch (start us, length us, event | category | flops | bytes accessed | tf_op | source)
XLA Modules:
  0.0 112.1 jit_solution(15758148026286314814)
XLA Ops:
  0.0 0.0 copy-start
  0.0 0.7 copy-done
  0.7 0.0 copy-start.1
  0.7 0.7 copy-done.1
  1.4 0.0 copy-start.2
  1.4 0.7 copy-done.2
  2.0 108.1 %shard_map.64 = f32[16,32,2048]{2,1,0:T(8,128)S(1)} custom-call(f32[128,16,512]{2,1,0:T(8,128)} %v_hbm.1, bf16[8,256,1152]{2,1,0:T(8,128)(2,1)} %constant.4.clone.w_hbm, bf16[2,8,2048,256]{3,2,1,0:T(8,128)(2,1)} %constant.5.clone.t_hbm, f32[1,128]{1,0:T(1,128)S(1)} %bitcast.4, f32[1,128]{1,0:T(1,128)S(1)} %bitcast.5, f32[1,2048]{1,0:T(1,128)S(1)} %bitcast.3), custom_call_target="tpu_custom_call" | custom-call | tf_op jit(solution)/shard_map/pallas_call | solution.py:267
  110.1 2.0 %copy.8 = f32[16,32,2048]{2,1,0:T(8,128)} copy(f32[16,32,2048]{2,1,0:T(8,128)S(1)} %shard_map.64) | data formatting | bytes 8388608
Async XLA Ops:
  0.0 0.7 copy-start
  0.7 0.7 copy-start.1
  1.4 0.7 copy-start.2
where the time goes:
time: 113 us; the launch traced here: 112 us
  Pallas kernels  108 us (96%)
  local copies, waits for them, and re-layouts  4.02 us (4%)
    pallas_call x1, Pallas kernels, transformed(): pl.pallas_call(functools.partial(kernel, (rows, cols, chunks, per, 1, 2))...  108 us
    unnamed x7, local copies, waits for them, and re-layouts  4.02 us

commit v1 on v0

v1 whole, which is shorter than its diff:
```python
import functools

import jax
import jax.numpy as jnp
import numpy as np
from jax import lax
from jax.experimental import pallas as pl
from jax.experimental.pallas import tpu as pltpu
from jax.sharding import PartitionSpec as P

SUB = 8
MESH = pl.DeviceIdType.MESH


def mode_table(count):
    rank = jnp.arange(count)
    angle = 2.0 * jnp.pi / count * (rank[:, None] * rank[None, :] % count).astype(jnp.float32)
    return (jnp.cos(angle) + jnp.sin(angle)) * count ** (-0.5)


def along_dim(values, dim):
    moved = jnp.tensordot(
        values, mode_table(values.shape[dim]), axes=([dim], [0]), precision=lax.Precision.HIGHEST
    )
    return jnp.moveaxis(moved, -1, dim)


def fixed_table(count):
    rank = np.arange(count)
    angle = 2.0 * np.pi / count * (rank[:, None] * rank[None, :] % count)
    return ((np.cos(angle) + np.sin(angle)) * count ** (-0.5)).astype(np.float32)


def halves(table):
    high = table.astype(jnp.bfloat16)
    low = (table - high.astype(np.float32)).astype(jnp.bfloat16)
    return high, low


def split(values):
    high = values.astype(jnp.bfloat16)
    low = (values - high.astype(jnp.float32)).astype(jnp.bfloat16)
    return high, low


def product(a, b):
    return jnp.dot(a, b, preferred_element_type=jnp.float32)


def flipped(index, mask):
    out = index
    bit = 1
    while bit <= mask:
        if mask & bit:
            out = out + bit * (1 - 2 * ((index // bit) % 2))
        bit *= 2
    return out


def kernel(
    dims, v_hbm, w_hbm, t_hbm, sx_hbm, sy_hbm, sz_hbm, out_ref,
    v, w, t, v_parts, xs, rbuf, ybuf, zbuf, lhs, factors, sx_row, sy_row, sz_ref, sx_col, sy_col,
    load_sem, v_sem, row_send, row_recv, first_recv, col_send, col_recv, last_recv,
):
    rows, cols, chunks, per, lag, lanes = dims
    part_y, part_z = v.shape[1], v.shape[2]
    grid_x, grid_y = v.shape[0], rbuf.shape[1]
    share_y, grid_z = zbuf.shape[1], zbuf.shape[2]
    tiles, tile = t.shape[1], t.shape[3]
    r, c = lax.axis_index("row"), lax.axis_index("col")
    spans = [pl.ds(p * lanes, lanes) for p in range(part_z // lanes)]

    load_w = pltpu.make_async_copy(w_hbm.at[0], w.at[0], load_sem.at[1])
    load_rest = pltpu.make_async_copy(w_hbm.at[pl.ds(1, chunks - 1)], w.at[pl.ds(1, chunks - 1)], load_sem.at[2])
    load_t = pltpu.make_async_copy(t_hbm, t, load_sem.at[0])
    load_v = [
        pltpu.make_async_copy(v_hbm.at[:, :, span], v.at[:, :, span], v_sem.at[p])
        for p, span in enumerate(spans)
    ]
    load_symbols = [
        pltpu.make_async_copy(source, target, load_sem.at[3 + n])
        for n, (source, target) in enumerate(((sx_hbm, sx_row), (sy_hbm, sy_row), (sz_hbm, sz_ref)))
    ]
    half = cols // 2
    side = c // half
    row_masks = sorted(range(1, rows), key=lambda m: (-bin(m // 2).count("1"), m))
    row_peers = [flipped(r, m) for m in row_masks]
    near = [flipped(c, m) for m in range(1, half)]
    across = [(half + j) * (1 - side) + (half - 1 - j) * side for j in range(half)]
    col_peers = near + across
    depth = (half - 1 - c) * (1 - side) + (c - half) * side
    col_marks = list(range(half - 1)) + [half - 1 + depth] * half

    barrier = pltpu.get_barrier_semaphore()
    for s in row_peers:
        pl.semaphore_signal(barrier, inc=1, device_id=(s, c), device_id_type=MESH)
    for s in col_peers:
        pl.semaphore_signal(barrier, inc=1, device_id=(r, s), device_id_type=MESH)
    load_w.start()
    for load in load_v + load_symbols:
        load.start()

    step = SUB * SUB
    whole = pl.ds(0, part_z)
    piece = part_z // 2 if part_z % 256 == 0 else part_z
    ends = [pl.ds(q * piece, piece) for q in range(part_z // piece)]

    def split_parts(span):
        def part_loop(i, carry):
            for g in range(part_y // SUB):
                block = v[pl.ds(i * SUB, SUB), g * SUB:(g + 1) * SUB, span].reshape(step, lanes)
                high, low = split(block)
                v_parts[g, 0, pl.ds(pl.multiple_of(i * step, step), step), span] = high
                v_parts[g, 1, pl.ds(pl.multiple_of(i * step, step), step), span] = low
            return carry

        lax.fori_loop(0, grid_x // SUB, part_loop, 0)

    def x_stage(k, span):
        m, depth = rows * per * SUB, grid_x * SUB
        for g in range(part_y // SUB):
            both = product(w[k, :2 * m, :depth], v_parts[g, 0, :, span])
            sums = both[:m] + both[m:] + product(w[k, :m, :depth], v_parts[g, 1, :, span])
            xs[k, :, g * SUB:(g + 1) * SUB, span] = sums.reshape(rows * per, SUB, span.size)

    def own_rows():
        return pl.ds(pl.multiple_of(r * part_y, SUB), part_y)

    def row_stage(k, span, recv):
        for i in range(per):
            for s in row_peers:
                pltpu.make_async_remote_copy(
                    src_ref=xs.at[k, s * per + i, :, span],
                    dst_ref=rbuf.at[k * per + i, own_rows(), span],
                    send_sem=row_send.at[k], recv_sem=recv.at[i],
                    device_id=(s, c), device_id_type=MESH,
                ).start()
        rbuf[pl.ds(k * per, per), own_rows(), span] = xs[k, pl.ds(r * per, per), :, span]

    def y_plane(k, i, span, recv):
        came = rbuf.at[k * per + i, pl.ds(0, grid_y - part_y), span]
        pltpu.make_async_copy(came, came, recv.at[i]).wait()
        high, low = split(rbuf[k * per + i, :, span])
        both = product(w[0, :2 * grid_y, grid_x * SUB:], high)
        ybuf[k, i, :, span] = both[:grid_y] + both[grid_y:] + product(w[0, :grid_y, grid_x * SUB:], low)

    def col_stage(k, i, span, recv):
        at = pl.ds(pl.multiple_of(c * part_z + span.start, 128), span.size)
        for s, mark in zip(col_peers, col_marks):
            pltpu.make_async_remote_copy(
                src_ref=ybuf.at[k, i, pl.ds(pl.multiple_of(s * share_y, SUB), share_y), span],
                dst_ref=zbuf.at[k * per + i, :, at],
                send_sem=col_send.at[k], recv_sem=recv.at[mark],
                device_id=(r, s), device_id_type=MESH,
            ).start()

    def y_stage(k, span, recv):
        for i in range(per):
            y_plane(k, i, span, recv)
            col_stage(k, i, span, col_recv.at[k])

    def last_y_stage(k, recv):
        for i in range(per):
            y_plane(k, i, whole, recv)
        for q, span in enumerate(ends):
            for i in range(per):
                col_stage(k, i, span, last_recv.at[q])

    def own_z(k):
        zbuf[pl.ds(k * per, per), :, pl.ds(pl.multiple_of(c * part_z, 128), part_z)] = (
            ybuf[k, :, pl.ds(pl.multiple_of(c * share_y, SUB), share_y), :]
        )

    def col_wait(k, m):
        came = zbuf.at[pl.ds(k * per, per), :, pl.ds(0, part_z)]
        pltpu.make_async_copy(came, came, col_recv.at[k, m]).wait()

    def factor_parts(k, n):
        y_part = sy_col[pl.ds(pl.multiple_of(c * share_y, SUB), share_y), :]
        z_part = sz_ref[:, pl.ds(pl.multiple_of(n * tile, tile), tile)]
        plane = jnp.concatenate([y_part] * (tile // 128), axis=1) + z_part
        for i in range(per):
            x_part = sx_col[pl.ds(r * chunks * per + k * per + i, 1), :]
            symbol = jnp.concatenate([x_part] * (tile // 128), axis=1) + plane
            yield i, (1.0 - 0.2 * symbol) / (1.0 + 0.2 * symbol)

    size = per * share_y

    def scaled(k, n, sums):
        for i, factor in factor_parts(k, n):
            out_ref[k * per + i, :, pl.ds(pl.multiple_of(n * tile, tile), tile)] = (
                sums[i * share_y:(i + 1) * share_y] * factor
            )

    def z_stage(k):
        for m in range(len(col_peers)):
            col_wait(k, m)
        high, low = split(zbuf[pl.ds(k * per, per)].reshape(size, grid_z))
        lhs[:size] = high
        lhs[size:] = low

        def tile_loop(n, carry):
            both = product(lhs[...], t[0, n])
            scaled(k, n, both[:size] + both[size:] + product(lhs[:size], t[1, n]))
            return carry

        lax.fori_loop(0, tiles, tile_loop, 0, unroll=2)

    def z_part(k, start, count, finish=None):
        span = pl.ds(pl.multiple_of(start, 128), count)
        high, low = split(zbuf[pl.ds(k * per, per), :, span].reshape(size, count))
        lhs[:size, :count] = high
        lhs[size:, :count] = low

        def tile_loop(n, carry):
            both = product(lhs[:, :count], t[0, n, span, :])
            sums = both[:size] + both[size:] + product(lhs[:size, :count], t[1, n, span, :])
            at = pl.ds(pl.multiple_of(n * tile, tile), tile)
            if count < grid_z // 2:
                sums = sums + out_ref[pl.ds(k * per, per), :, at].reshape(size, tile)
            if finish is None:
                out_ref[pl.ds(k * per, per), :, at] = sums.reshape(per, share_y, tile)
            else:
                finish(k, n, sums)
            return carry

        lax.fori_loop(0, tiles, tile_loop, 0, unroll=4)

    def prepare(k):
        def tile_loop(n, carry):
            for i, factor in factor_parts(k, n):
                factors[i, :, pl.ds(pl.multiple_of(n * tile, tile), tile)] = factor
            return carry

        lax.fori_loop(0, tiles, tile_loop, 0)

    def multiplied(k, n, sums):
        at = pl.ds(pl.multiple_of(n * tile, tile), tile)
        out_ref[pl.ds(k * per, per), :, at] = sums.reshape(per, share_y, tile) * factors[:, :, at]

    def last_wait(q, m):
        came = zbuf.at[pl.ds((chunks - 1) * per, per), :, pl.ds(0, piece)]
        pltpu.make_async_copy(came, came, last_recv.at[q, m]).wait()

    def last_z_stages():
        before, last = chunks - 2, chunks - 1
        for m in range(len(near)):
            col_wait(before, m)
        z_part(before, side * half * part_z, half * part_z)
        for j in range(half - 1):
            col_wait(before, len(near) + j)
            z_part(before, across[j] * part_z, part_z)
        for m in range(len(near)):
            for q in range(len(ends)):
                last_wait(q, m)
        z_part(last, side * half * part_z, half * part_z)
        prepare(last)
        for j in range(half - 1):
            for q in range(len(ends)):
                last_wait(q, len(near) + j)
            z_part(last, across[j] * part_z, part_z)
        col_wait(before, len(col_peers) - 1)
        z_part(before, across[-1] * part_z, part_z, scaled)
        for q, span in enumerate(ends):
            last_wait(q, len(col_peers) - 1)
            z_part(last, across[-1] * part_z + span.start, piece, multiplied if q == len(ends) - 1 else None)

    for p, span in enumerate(spans):
        load_v[p].wait()
        split_parts(span)
        if p == 0:
            load_w.wait()
        x_stage(0, span)
        if p == 0:
            pl.semaphore_wait(barrier, len(row_peers) + len(col_peers))
        row_stage(0, span, first_recv.at[p])
    load_rest.start()
    load_t.start()
    y_stage(0, spans[0], first_recv.at[0])
    load_rest.wait()
    x_stage(1, whole)
    row_stage(1, whole, row_recv.at[1])
    for p, span in enumerate(spans[1:]):
        y_stage(0, span, first_recv.at[p + 1])
    own_z(0)
    for load in load_symbols:
        load.wait()
    for ref, column in ((sx_row, sx_col), (sy_row, sy_col)):
        column[...] = jnp.broadcast_to(ref[...], (128, ref.shape[1])).T

    def loop(k, carry):
        @pl.when(k < chunks)
        def _():
            x_stage(k, whole)
            row_stage(k, whole, row_recv.at[k])

        @pl.when(k < chunks)
        def _():
            y_stage(k - 1, whole, row_recv.at[k - 1])
            own_z(k - 1)

        @pl.when(k == chunks)
        def _():
            last_y_stage(chunks - 1, row_recv.at[chunks - 1])
            own_z(chunks - 1)

        @pl.when(k == lag + 1)
        def _():
            load_t.wait()

        @pl.when(k >= lag + 1)
        def _():
            z_stage(k - 1 - lag)

        return carry

    lax.fori_loop(2, chunks + lag - 1, loop, 0)
    last_z_stages()

    def drain(k, carry):
        sent = rbuf.at[pl.ds(k * per, per), pl.ds(0, grid_y - part_y), :]
        pltpu.make_async_copy(sent, sent, row_send.at[k]).wait()
        sent = zbuf.at[pl.ds(k * per, per), :, pl.ds(0, grid_z - part_z)]
        pltpu.make_async_copy(sent, sent, col_send.at[k]).wait()
        return carry

    lax.fori_loop(0, chunks, drain, 0)


def transformed(rows, cols, velocity, symbol_x, symbol_y, symbol_z):
    grid_x, part_y, part_z = velocity.shape
    grid_y, grid_z = part_y * rows, part_z * cols
    share_x, share_y = grid_x // rows, grid_y // cols
    chunks = min(8, share_x)
    per = share_x // chunks
    tile = 256
    hx, hy, hz = fixed_table(grid_x), fixed_table(grid_y), fixed_table(grid_z)
    order = np.arange(grid_x).reshape(rows, chunks, per).transpose(1, 0, 2).reshape(chunks, rows * per)
    w = np.stack([np.kron(hx[o], np.eye(SUB, dtype=np.float32)) for o in order])
    w = np.concatenate(halves(w), axis=1)
    h = np.concatenate(halves(hy), axis=0)
    t = np.stack(halves(hz)).reshape(2, grid_z, grid_z // tile, tile).transpose(0, 2, 1, 3)
    held = np.zeros((chunks, max(w.shape[1], h.shape[0]), w.shape[2] + h.shape[1]), w.dtype)
    held[:, :w.shape[1], :w.shape[2]] = w
    held[0, :h.shape[0], w.shape[2]:] = h
    f32, bf16 = jnp.float32, jnp.bfloat16
    hbm = pl.BlockSpec(memory_space=pltpu.HBM)
    vmem = pl.BlockSpec(memory_space=pltpu.VMEM)
    return pl.pallas_call(
        functools.partial(kernel, (rows, cols, chunks, per, 2, 128)),
        out_shape=jax.ShapeDtypeStruct((share_x, share_y, grid_z), f32),
        in_specs=[hbm] * 6,
        out_specs=vmem,
        scratch_shapes=[
            pltpu.VMEM(velocity.shape, f32),
            pltpu.VMEM(held.shape, bf16),
            pltpu.VMEM(t.shape, bf16),
            pltpu.VMEM((part_y // SUB, 2, grid_x * SUB, part_z), bf16),
            pltpu.VMEM((chunks, rows * per, part_y, part_z), f32),
            pltpu.VMEM((share_x, grid_y, part_z), f32),
            pltpu.VMEM((chunks, per, grid_y, part_z), f32),
            pltpu.VMEM((share_x, share_y, grid_z), f32),
            pltpu.VMEM((2 * per * share_y, grid_z), bf16),
            pltpu.VMEM((per, share_y, grid_z), f32),
            pltpu.VMEM((1, grid_x), f32),
            pltpu.VMEM((1, grid_y), f32),
            pltpu.VMEM((1, grid_z), f32),
            pltpu.VMEM((grid_x, 128), f32),
            pltpu.VMEM((grid_y, 128), f32),
            pltpu.SemaphoreType.DMA((6,)),
            pltpu.SemaphoreType.DMA((part_z // 128,)),
            pltpu.SemaphoreType.DMA((chunks,)),
            pltpu.SemaphoreType.DMA((chunks, per)),
            pltpu.SemaphoreType.DMA((part_z // 128, per)),
            pltpu.SemaphoreType.DMA((chunks,)),
            pltpu.SemaphoreType.DMA((chunks, cols - 1)),
            pltpu.SemaphoreType.DMA((2, cols - 1)),
        ],
        compiler_params=pltpu.CompilerParams(
            collective_id=0, has_side_effects=True, vmem_limit_bytes=47 * 2**20
        ),
    )(velocity, jnp.asarray(held), jnp.asarray(np.ascontiguousarray(t)),
      *(pltpu.with_memory_space_constraint(symbol[None, :], pltpu.HBM) for symbol in (symbol_x, symbol_y, symbol_z)))


def fits(rows, cols, shape):
    grid_x, part_y, part_z = shape
    grid_z = part_z * cols
    held = 7 * grid_x * part_y * part_z * 4 + 4 * grid_z * grid_z + 4 * (grid_x * SUB) ** 2
    even = rows & (rows - 1) == 0 and cols & (cols - 1) == 0 and cols > 1 and grid_x % (8 * rows) == 0
    return even and part_y % SUB == 0 and part_z % 128 == 0 and (part_y * rows) % (SUB * cols) == 0 and held < 54 * 2**20


def local(rows, cols, velocity, symbol_x, symbol_y, symbol_z):
    if fits(rows, cols, velocity.shape):
        return transformed(rows, cols, velocity, symbol_x, symbol_y, symbol_z)
    part_values = along_dim(velocity, 0)
    part_values = lax.all_to_all(part_values, "row", split_axis=0, concat_axis=1, tiled=True)
    pencil_values = along_dim(part_values, 1)
    pencil_values = lax.all_to_all(pencil_values, "col", split_axis=1, concat_axis=2, tiled=True)
    pencil_values = along_dim(pencil_values, 2)
    share_x = pencil_values.shape[0]
    part_x = lax.dynamic_slice_in_dim(symbol_x, lax.axis_index("row") * share_x, share_x)
    share_y = pencil_values.shape[1]
    part_y = lax.dynamic_slice_in_dim(symbol_y, lax.axis_index("col") * share_y, share_y)
    symbol = part_x[:, None, None] + part_y[None, :, None] + symbol_z[None, None, :]
    return pencil_values * ((1.0 - 0.2 * symbol) / (1.0 + 0.2 * symbol))


def solution(mesh):
    placed = (P(None, "row", "col"), P(), P(), P())
    return jax.shard_map(
        functools.partial(local, mesh.shape["row"], mesh.shape["col"]),
        mesh=mesh, in_specs=placed, out_specs=P("row", "col", None), check_vma=False,
    )
```

time: 113 us -> 108 us (0.956)
  Pallas kernels: 108 us -> 106 us
  local copies, waits for them, and re-layouts: 4.02 us -> 2.02 us
    pallas_call x1, Pallas kernels: 108 us -> 106 us  [transformed(): pl.pallas_call(functools.partial(kernel, (rows, cols, chunks, per, 2, 128...]
    unnamed x7 -> x1, local copies, waits for them, and re-layouts: 4.02 us -> 2.02 us
where the time goes in v1:
time: 108 us
  Pallas kernels  106 us (98%)
  local copies, waits for them, and re-layouts  2.02 us (2%)
    pallas_call x1, Pallas kernels, transformed(): pl.pallas_call(functools.partial(kernel, (rows, cols, chunks, per, 2, 128...  106 us

profile of v1, /device:TPU:0, one launch (start us, length us, event | category | flops | bytes accessed | tf_op | source)
XLA Modules:
  0.0 107.9 jit_solution(15647777531802128314)
XLA Ops:
  0.0 105.9 %shard_map.64 = f32[16,32,2048]{2,1,0:T(8,128)S(1)} custom-call(f32[128,16,512]{2,1,0:T(8,128)} %v_hbm.1, bf16[8,256,1152]{2,1,0:T(8,128)(2,1)} %constant.4.clone.w_hbm, bf16[2,8,2048,256]{3,2,1,0:T(8,128)(2,1)} %constant.5.clone.t_hbm, f32[1,128]{1,0:T(1,128)} %bitcast.4, f32[1,128]{1,0:T(1,128)} %bitcast.5, f32[1,2048]{1,0:T(1,128)} %bitcast.3), custom_call_target="tpu_custom_call" | custom-call | tf_op jit(solution)/shard_map/pallas_call | solution.py:349
  105.9 2.0 %copy.8 = f32[16,32,2048]{2,1,0:T(8,128)} copy(f32[16,32,2048]{2,1,0:T(8,128)S(1)} %shard_map.64) | data formatting | bytes 8388608

commit v2 on v1

--- a/solution.py
+++ b/solution.py
@@ -86,10 +86,11 @@
     row_masks = sorted(range(1, rows), key=lambda m: (-bin(m // 2).count("1"), m))
     row_peers = [flipped(r, m) for m in row_masks]
     near = [flipped(c, m) for m in range(1, half)]
-    across = [(half + j) * (1 - side) + (half - 1 - j) * side for j in range(half)]
+    across = [(half + j) * (1 - side) + (half - 1 - j) * side for j in reversed(range(half))]
     col_peers = near + across
     depth = (half - 1 - c) * (1 - side) + (c - half) * side
-    col_marks = list(range(half - 1)) + [half - 1 + depth] * half
+    marks = list(range(half - 1)) + [2 * half - 2 - depth] * half
+    col_targets = list(zip(col_peers, marks))
 
     barrier = pltpu.get_barrier_semaphore()
     for s in row_peers:
@@ -144,9 +145,9 @@
         both = product(w[0, :2 * grid_y, grid_x * SUB:], high)
         ybuf[k, i, :, span] = both[:grid_y] + both[grid_y:] + product(w[0, :grid_y, grid_x * SUB:], low)
 
-    def col_stage(k, i, span, recv):
+    def col_stage(k, i, span, recv, targets):
         at = pl.ds(pl.multiple_of(c * part_z + span.start, 128), span.size)
-        for s, mark in zip(col_peers, col_marks):
+        for s, mark in targets:
             pltpu.make_async_remote_copy(
                 src_ref=ybuf.at[k, i, pl.ds(pl.multiple_of(s * share_y, SUB), share_y), span],
                 dst_ref=zbuf.at[k * per + i, :, at],
@@ -157,14 +158,15 @@
     def y_stage(k, span, recv):
         for i in range(per):
             y_plane(k, i, span, recv)
-            col_stage(k, i, span, col_recv.at[k])
+            col_stage(k, i, span, col_recv.at[k], col_targets)
 
     def last_y_stage(k, recv):
         for i in range(per):
             y_plane(k, i, whole, recv)
-        for q, span in enumerate(ends):
-            for i in range(per):
-                col_stage(k, i, span, last_recv.at[q])
+        for target in col_targets:
+            for q, span in enumerate(ends):
+                for i in range(per):
+                    col_stage(k, i, span, last_recv.at[q], [target])
 
     def own_z(k):
         zbuf[pl.ds(k * per, per), :, pl.ds(pl.multiple_of(c * part_z, 128), part_z)] = (

time: 108 us -> 103 us (0.954)
  Pallas kernels: 106 us -> 101 us
    pallas_call x1, Pallas kernels: 106 us -> 101 us  [transformed(): pl.pallas_call(functools.partial(kernel, (rows, cols, chunks, per, 2, 128...]
where the time goes in v2:
time: 103 us
  Pallas kernels  101 us (98%)
  local copies, waits for them, and re-layouts  2.02 us (2%)
    pallas_call x1, Pallas kernels, transformed(): pl.pallas_call(functools.partial(kernel, (rows, cols, chunks, per, 2, 128...  101 us

profile of v2, /device:TPU:0, one launch (start us, length us, event | category | flops | bytes accessed | tf_op | source)
XLA Modules:
  0.0 102.9 jit_solution(4191266212985060906)
XLA Ops:
  0.0 100.9 %shard_map.64 = f32[16,32,2048]{2,1,0:T(8,128)S(1)} custom-call(f32[128,16,512]{2,1,0:T(8,128)} %v_hbm.1, bf16[8,256,1152]{2,1,0:T(8,128)(2,1)} %constant.4.clone.w_hbm, bf16[2,8,2048,256]{3,2,1,0:T(8,128)(2,1)} %constant.5.clone.t_hbm, f32[1,128]{1,0:T(1,128)} %bitcast.4, f32[1,128]{1,0:T(1,128)} %bitcast.5, f32[1,2048]{1,0:T(1,128)} %bitcast.3), custom_call_target="tpu_custom_call" | custom-call | tf_op jit(solution)/shard_map/pallas_call | solution.py:351
  100.9 2.0 %copy.8 = f32[16,32,2048]{2,1,0:T(8,128)} copy(f32[16,32,2048]{2,1,0:T(8,128)S(1)} %shard_map.64) | data formatting | bytes 8388608

commit v3 on v2

--- a/solution.py
+++ b/solution.py
@@ -59,8 +59,8 @@
 
 def kernel(
     dims, v_hbm, w_hbm, t_hbm, sx_hbm, sy_hbm, sz_hbm, out_ref,
-    v, w, t, v_parts, xs, rbuf, ybuf, zbuf, lhs, factors, sx_row, sy_row, sz_ref, sx_col, sy_col,
-    load_sem, v_sem, row_send, row_recv, first_recv, col_send, col_recv, last_recv,
+    v, w, t, v_parts, xs, rbuf, ybuf, zbuf, lhs, factors, raw_in, raw_all, raw_y, sx_row, sy_row, sz_ref, sx_col, sy_col,
+    load_sem, v_sem, row_send, row_recv, first_recv, col_send, col_recv, last_recv, raw_send, raw_recv, raw_near,
 ):
     rows, cols, chunks, per, lag, lanes = dims
     part_y, part_z = v.shape[1], v.shape[2]
@@ -88,6 +88,7 @@
     near = [flipped(c, m) for m in range(1, half)]
     across = [(half + j) * (1 - side) + (half - 1 - j) * side for j in reversed(range(half))]
     col_peers = near + across
+    mirror = cols - 1 - c
     depth = (half - 1 - c) * (1 - side) + (c - half) * side
     marks = list(range(half - 1)) + [2 * half - 2 - depth] * half
     col_targets = list(zip(col_peers, marks))
@@ -103,8 +104,11 @@
 
     step = SUB * SUB
     whole = pl.ds(0, part_z)
-    piece = part_z // 2 if part_z % 256 == 0 else part_z
-    ends = [pl.ds(q * piece, piece) for q in range(part_z // piece)]
+    ends, done = [], 0
+    while done < part_z:
+        left = part_z - done
+        ends.append(pl.ds(done, left // 2 if left % 256 == 0 and len(ends) < 2 else left))
+        done += ends[-1].size
 
     def split_parts(span):
         def part_loop(i, carry):
@@ -133,7 +137,7 @@
                 pltpu.make_async_remote_copy(
                     src_ref=xs.at[k, s * per + i, :, span],
                     dst_ref=rbuf.at[k * per + i, own_rows(), span],
-                    send_sem=row_send.at[k], recv_sem=recv.at[i],
+                    send_sem=row_send, recv_sem=recv.at[i],
                     device_id=(s, c), device_id_type=MESH,
                 ).start()
         rbuf[pl.ds(k * per, per), own_rows(), span] = xs[k, pl.ds(r * per, per), :, span]
@@ -151,14 +155,49 @@
             pltpu.make_async_remote_copy(
                 src_ref=ybuf.at[k, i, pl.ds(pl.multiple_of(s * share_y, SUB), share_y), span],
                 dst_ref=zbuf.at[k * per + i, :, at],
-                send_sem=col_send.at[k], recv_sem=recv.at[mark],
+                send_sem=col_send, recv_sem=recv.at[mark],
                 device_id=(r, s), device_id_type=MESH,
             ).start()
 
-    def y_stage(k, span, recv):
+    def y_stage(k, span, recv, raw=False):
         for i in range(per):
             y_plane(k, i, span, recv)
-            col_stage(k, i, span, col_recv.at[k], col_targets)
+            near_only = raw and i == per - 1
+            col_stage(k, i, span, col_recv.at[k], col_targets[:len(near)] if near_only else col_targets)
+
+    def raw_stage():
+        for s in range(rows):
+            pltpu.make_async_remote_copy(
+                src_ref=xs.at[0, s * per + per - 1, :, spans[0]], dst_ref=raw_in.at[s],
+                send_sem=raw_send.at[0], recv_sem=raw_recv.at[0],
+                device_id=(r, mirror), device_id_type=MESH,
+            ).start()
+
+    def raw_row_stage():
+        pltpu.make_async_copy(raw_in, raw_in, raw_recv.at[0]).wait()
+        for s in row_peers:
+            pltpu.make_async_remote_copy(
+                src_ref=raw_in.at[s], dst_ref=raw_all.at[own_rows(), :],
+                send_sem=raw_send.at[1], recv_sem=raw_recv.at[1],
+                device_id=(s, c), device_id_type=MESH,
+            ).start()
+        raw_all[own_rows(), :] = raw_in[r]
+
+    def raw_y_stage():
+        came = raw_all.at[pl.ds(0, grid_y - part_y), :]
+        pltpu.make_async_copy(came, came, raw_recv.at[1]).wait()
+        high, low = split(raw_all[...])
+        both = product(w[0, :2 * grid_y, grid_x * SUB:], high)
+        raw_y[...] = both[:grid_y] + both[grid_y:] + product(w[0, :grid_y, grid_x * SUB:], low)
+        at = pl.ds(pl.multiple_of(mirror * part_z, 128), lanes)
+        for m, s in enumerate(near):
+            pltpu.make_async_remote_copy(
+                src_ref=raw_y.at[pl.ds(pl.multiple_of(s * share_y, SUB), share_y), :],
+                dst_ref=zbuf.at[per - 1, :, at],
+                send_sem=raw_send.at[2], recv_sem=raw_near.at[m],
+                device_id=(r, s), device_id_type=MESH,
+            ).start()
+        zbuf[per - 1, :, at] = raw_y[pl.ds(pl.multiple_of(c * share_y, SUB), share_y), :]
 
     def last_y_stage(k, recv):
         for i in range(per):
@@ -194,21 +233,7 @@
                 sums[i * share_y:(i + 1) * share_y] * factor
             )
 
-    def z_stage(k):
-        for m in range(len(col_peers)):
-            col_wait(k, m)
-        high, low = split(zbuf[pl.ds(k * per, per)].reshape(size, grid_z))
-        lhs[:size] = high
-        lhs[size:] = low
-
-        def tile_loop(n, carry):
-            both = product(lhs[...], t[0, n])
-            scaled(k, n, both[:size] + both[size:] + product(lhs[:size], t[1, n]))
-            return carry
-
-        lax.fori_loop(0, tiles, tile_loop, 0, unroll=2)
-
-    def z_part(k, start, count, finish=None):
+    def z_part(k, start, count, finish=None, first=False):
         span = pl.ds(pl.multiple_of(start, 128), count)
         high, low = split(zbuf[pl.ds(k * per, per), :, span].reshape(size, count))
         lhs[:size, :count] = high
@@ -218,7 +243,7 @@
             both = product(lhs[:, :count], t[0, n, span, :])
             sums = both[:size] + both[size:] + product(lhs[:size, :count], t[1, n, span, :])
             at = pl.ds(pl.multiple_of(n * tile, tile), tile)
-            if count < grid_z // 2:
+            if not first:
                 sums = sums + out_ref[pl.ds(k * per, per), :, at].reshape(size, tile)
             if finish is None:
                 out_ref[pl.ds(k * per, per), :, at] = sums.reshape(per, share_y, tile)
@@ -226,7 +251,7 @@
                 finish(k, n, sums)
             return carry
 
-        lax.fori_loop(0, tiles, tile_loop, 0, unroll=4)
+        lax.fori_loop(0, tiles, tile_loop, 0, unroll=8 if count <= 256 else 4)
 
     def prepare(k):
         def tile_loop(n, carry):
@@ -241,22 +266,41 @@
         out_ref[pl.ds(k * per, per), :, at] = sums.reshape(per, share_y, tile) * factors[:, :, at]
 
     def last_wait(q, m):
-        came = zbuf.at[pl.ds((chunks - 1) * per, per), :, pl.ds(0, piece)]
+        came = zbuf.at[pl.ds((chunks - 1) * per, per), :, pl.ds(0, ends[q].size)]
         pltpu.make_async_copy(came, came, last_recv.at[q, m]).wait()
 
-    def last_z_stages():
+    def own_stage(k):
+        for m in range(len(near)):
+            col_wait(k, m)
+        z_part(k, side * half * part_z, half * part_z, first=True)
+
+    def across_stage(k):
+        @pl.when(k == 0)
+        def _():
+            for m in range(len(near), len(col_peers)):
+                came = zbuf.at[0, :, pl.ds(0, per * part_z - lanes)]
+                pltpu.make_async_copy(came, came, col_recv.at[0, m]).wait()
+            for m in range(len(near)):
+                came = zbuf.at[0, :, pl.ds(0, lanes)]
+                pltpu.make_async_copy(came, came, raw_near.at[m]).wait()
+
+        @pl.when(k > 0)
+        def _():
+            for m in range(len(near), len(col_peers)):
+                col_wait(k, m)
+
+        z_part(k, (1 - side) * half * part_z, half * part_z, scaled)
+
+    def last_stages():
         before, last = chunks - 2, chunks - 1
         for m in range(len(near)):
-            col_wait(before, m)
-        z_part(before, side * half * part_z, half * part_z)
+            for q in range(len(ends)):
+                last_wait(q, m)
+        z_part(last, side * half * part_z, half * part_z, first=True)
+        prepare(last)
         for j in range(half - 1):
             col_wait(before, len(near) + j)
             z_part(before, across[j] * part_z, part_z)
-        for m in range(len(near)):
-            for q in range(len(ends)):
-                last_wait(q, m)
-        z_part(last, side * half * part_z, half * part_z)
-        prepare(last)
         for j in range(half - 1):
             for q in range(len(ends)):
                 last_wait(q, len(near) + j)
@@ -265,7 +309,7 @@
         z_part(before, across[-1] * part_z, part_z, scaled)
         for q, span in enumerate(ends):
             last_wait(q, len(col_peers) - 1)
-            z_part(last, across[-1] * part_z + span.start, piece, multiplied if q == len(ends) - 1 else None)
+            z_part(last, across[-1] * part_z + span.start, span.size, multiplied if q == len(ends) - 1 else None)
 
     for p, span in enumerate(spans):
         load_v[p].wait()
@@ -276,15 +320,18 @@
         if p == 0:
             pl.semaphore_wait(barrier, len(row_peers) + len(col_peers))
         row_stage(0, span, first_recv.at[p])
+        if p == 0:
+            raw_stage()
     load_rest.start()
     load_t.start()
-    y_stage(0, spans[0], first_recv.at[0])
+    y_stage(0, spans[0], first_recv.at[0], raw=True)
     load_rest.wait()
     x_stage(1, whole)
     row_stage(1, whole, row_recv.at[1])
     for p, span in enumerate(spans[1:]):
         y_stage(0, span, first_recv.at[p + 1])
     own_z(0)
+    raw_row_stage()
     for load in load_symbols:
         load.wait()
     for ref, column in ((sx_row, sx_col), (sy_row, sy_col)):
@@ -306,27 +353,35 @@
             last_y_stage(chunks - 1, row_recv.at[chunks - 1])
             own_z(chunks - 1)
 
-        @pl.when(k == lag + 1)
-        def _():
+        @pl.when(k == 2)
+        def _():
+            raw_y_stage()
             load_t.wait()
 
+        own_stage(k - lag)
+
         @pl.when(k >= lag + 1)
         def _():
-            z_stage(k - 1 - lag)
+            across_stage(k - 1 - lag)
 
         return carry
 
     lax.fori_loop(2, chunks + lag - 1, loop, 0)
-    last_z_stages()
-
-    def drain(k, carry):
-        sent = rbuf.at[pl.ds(k * per, per), pl.ds(0, grid_y - part_y), :]
-        pltpu.make_async_copy(sent, sent, row_send.at[k]).wait()
-        sent = zbuf.at[pl.ds(k * per, per), :, pl.ds(0, grid_z - part_z)]
-        pltpu.make_async_copy(sent, sent, col_send.at[k]).wait()
-        return carry
-
-    lax.fori_loop(0, chunks, drain, 0)
+    last_stages()
+
+    sent = rbuf.at[:, pl.ds(0, grid_y - part_y), :]
+    pltpu.make_async_copy(sent, sent, row_send).wait()
+    pltpu.make_async_copy(raw_in, raw_in, raw_send.at[0]).wait()
+    sent = raw_all.at[pl.ds(0, grid_y - part_y), :]
+    pltpu.make_async_copy(sent, sent, raw_send.at[1]).wait()
+    if near:
+        sent = raw_y.at[pl.ds(0, len(near) * share_y), :]
+        pltpu.make_async_copy(sent, sent, raw_send.at[2]).wait()
+    for sent in (
+        zbuf.at[pl.ds(1, grid_x // rows - 1), :, pl.ds(0, grid_z - part_z)],
+        zbuf.at[0, :, pl.ds(0, grid_z - part_z - half * lanes)],
+    ):
+        pltpu.make_async_copy(sent, sent, col_send).wait()
 
 
 def transformed(rows, cols, velocity, symbol_x, symbol_y, symbol_z):
@@ -364,6 +419,9 @@
             pltpu.VMEM((share_x, share_y, grid_z), f32),
             pltpu.VMEM((2 * per * share_y, grid_z), bf16),
             pltpu.VMEM((per, share_y, grid_z), f32),
+            pltpu.VMEM((rows, part_y, 128), f32),
+            pltpu.VMEM((grid_y, 128), f32),
+            pltpu.VMEM((grid_y, 128), f32),
             pltpu.VMEM((1, grid_x), f32),
             pltpu.VMEM((1, grid_y), f32),
             pltpu.VMEM((1, grid_z), f32),
@@ -371,12 +429,15 @@
             pltpu.VMEM((grid_y, 128), f32),
             pltpu.SemaphoreType.DMA((6,)),
             pltpu.SemaphoreType.DMA((part_z // 128,)),
-            pltpu.SemaphoreType.DMA((chunks,)),
+            pltpu.SemaphoreType.DMA,
             pltpu.SemaphoreType.DMA((chunks, per)),
             pltpu.SemaphoreType.DMA((part_z // 128, per)),
-            pltpu.SemaphoreType.DMA((chunks,)),
+            pltpu.SemaphoreType.DMA,
             pltpu.SemaphoreType.DMA((chunks, cols - 1)),
-            pltpu.SemaphoreType.DMA((2, cols - 1)),
+            pltpu.SemaphoreType.DMA((3, cols - 1)),
+            pltpu.SemaphoreType.DMA((3,)),
+            pltpu.SemaphoreType.DMA((2,)),
+            pltpu.SemaphoreType.DMA((max(1, cols // 2 - 1),)),
         ],
         compiler_params=pltpu.CompilerParams(
             collective_id=0, has_side_effects=True, vmem_limit_bytes=47 * 2**20
@@ -389,7 +450,8 @@
     grid_x, part_y, part_z = shape
     grid_z = part_z * cols
     held = 7 * grid_x * part_y * part_z * 4 + 4 * grid_z * grid_z + 4 * (grid_x * SUB) ** 2
-    even = rows & (rows - 1) == 0 and cols & (cols - 1) == 0 and cols > 1 and grid_x % (8 * rows) == 0
+    even = rows & (rows - 1) == 0 and cols & (cols - 1) == 0 and cols > 1 and grid_x % (16 * rows) == 0
+    even = even and grid_x * part_z <= 8 * rows * grid_z
     return even and part_y % SUB == 0 and part_z % 128 == 0 and (part_y * rows) % (SUB * cols) == 0 and held < 54 * 2**20
 
 

time: 103 us -> 102 us (level)
  Pallas kernels: 101 us -> 99.6 us
    pallas_call x1, Pallas kernels: 101 us -> 99.6 us  [transformed(): pl.pallas_call(functools.partial(kernel, (rows, cols, chunks, per, 2, 128...]
where the time goes in v3:
time: 102 us
  Pallas kernels  99.6 us (98%)
  local copies, waits for them, and re-layouts  2.02 us (2%)
    pallas_call x1, Pallas kernels, transformed(): pl.pallas_call(functools.partial(kernel, (rows, cols, chunks, per, 2, 128...  99.6 us

profile of v3, /device:TPU:0, one launch (start us, length us, event | category | flops | bytes accessed | tf_op | source)
XLA Modules:
  0.0 101.7 jit_solution(2588377834119095196)
XLA Ops:
  0.0 99.6 %shard_map.64 = f32[16,32,2048]{2,1,0:T(8,128)S(1)} custom-call(f32[128,16,512]{2,1,0:T(8,128)} %v_hbm.1, bf16[8,256,1152]{2,1,0:T(8,128)(2,1)} %constant.4.clone.w_hbm, bf16[2,8,2048,256]{3,2,1,0:T(8,128)(2,1)} %constant.5.clone.t_hbm, f32[1,128]{1,0:T(1,128)} %bitcast.4, f32[1,128]{1,0:T(1,128)} %bitcast.5, f32[1,2048]{1,0:T(1,128)} %bitcast.3), custom_call_target="tpu_custom_call" | custom-call | tf_op jit(solution)/shard_map/pallas_call | solution.py:406
  99.7 2.0 %copy.8 = f32[16,32,2048]{2,1,0:T(8,128)} copy(f32[16,32,2048]{2,1,0:T(8,128)S(1)} %shard_map.64) | data formatting | bytes 8388608

commit v4 on v3

--- a/solution.py
+++ b/solution.py
@@ -60,9 +60,10 @@
 def kernel(
     dims, v_hbm, w_hbm, t_hbm, sx_hbm, sy_hbm, sz_hbm, out_ref,
     v, w, t, v_parts, xs, rbuf, ybuf, zbuf, lhs, factors, raw_in, raw_all, raw_y, sx_row, sy_row, sz_ref, sx_col, sy_col,
-    load_sem, v_sem, row_send, row_recv, first_recv, col_send, col_recv, last_recv, raw_send, raw_recv, raw_near,
+    load_sem, v_sem, sent_sem, row_recv, first_recv, col_recv, last_recv, raw_recv, raw_near,
 ):
-    rows, cols, chunks, per, lag, lanes = dims
+    rows, cols, chunks, per, lag, lanes, raws = dims
+    raw = raws * lanes
     part_y, part_z = v.shape[1], v.shape[2]
     grid_x, grid_y = v.shape[0], rbuf.shape[1]
     share_y, grid_z = zbuf.shape[1], zbuf.shape[2]
@@ -73,9 +74,10 @@
     load_w = pltpu.make_async_copy(w_hbm.at[0], w.at[0], load_sem.at[1])
     load_rest = pltpu.make_async_copy(w_hbm.at[pl.ds(1, chunks - 1)], w.at[pl.ds(1, chunks - 1)], load_sem.at[2])
     load_t = pltpu.make_async_copy(t_hbm, t, load_sem.at[0])
+    groups = [pl.ds(g * SUB, SUB) for g in range(part_y // SUB)]
+    parts = [(group, spans[0]) for group in groups] + [(pl.ds(0, part_y), span) for span in spans[1:]]
     load_v = [
-        pltpu.make_async_copy(v_hbm.at[:, :, span], v.at[:, :, span], v_sem.at[p])
-        for p, span in enumerate(spans)
+        pltpu.make_async_copy(v_hbm.at[:, y, z], v.at[:, y, z], v_sem.at[p]) for p, (y, z) in enumerate(parts)
     ]
     load_symbols = [
         pltpu.make_async_copy(source, target, load_sem.at[3 + n])
@@ -110,9 +112,9 @@
         ends.append(pl.ds(done, left // 2 if left % 256 == 0 and len(ends) < 2 else left))
         done += ends[-1].size
 
-    def split_parts(span):
+    def split_parts(span, picked):
         def part_loop(i, carry):
-            for g in range(part_y // SUB):
+            for g in picked:
                 block = v[pl.ds(i * SUB, SUB), g * SUB:(g + 1) * SUB, span].reshape(step, lanes)
                 high, low = split(block)
                 v_parts[g, 0, pl.ds(pl.multiple_of(i * step, step), step), span] = high
@@ -121,9 +123,9 @@
 
         lax.fori_loop(0, grid_x // SUB, part_loop, 0)
 
-    def x_stage(k, span):
+    def x_stage(k, span, picked):
         m, depth = rows * per * SUB, grid_x * SUB
-        for g in range(part_y // SUB):
+        for g in picked:
             both = product(w[k, :2 * m, :depth], v_parts[g, 0, :, span])
             sums = both[:m] + both[m:] + product(w[k, :m, :depth], v_parts[g, 1, :, span])
             xs[k, :, g * SUB:(g + 1) * SUB, span] = sums.reshape(rows * per, SUB, span.size)
@@ -137,7 +139,7 @@
                 pltpu.make_async_remote_copy(
                     src_ref=xs.at[k, s * per + i, :, span],
                     dst_ref=rbuf.at[k * per + i, own_rows(), span],
-                    send_sem=row_send, recv_sem=recv.at[i],
+                    send_sem=sent_sem, recv_sem=recv.at[i],
                     device_id=(s, c), device_id_type=MESH,
                 ).start()
         rbuf[pl.ds(k * per, per), own_rows(), span] = xs[k, pl.ds(r * per, per), :, span]
@@ -155,21 +157,21 @@
             pltpu.make_async_remote_copy(
                 src_ref=ybuf.at[k, i, pl.ds(pl.multiple_of(s * share_y, SUB), share_y), span],
                 dst_ref=zbuf.at[k * per + i, :, at],
-                send_sem=col_send, recv_sem=recv.at[mark],
+                send_sem=sent_sem, recv_sem=recv.at[mark],
                 device_id=(r, s), device_id_type=MESH,
             ).start()
 
-    def y_stage(k, span, recv, raw=False):
+    def y_stage(k, span, recv, crossed=False):
         for i in range(per):
             y_plane(k, i, span, recv)
-            near_only = raw and i == per - 1
+            near_only = crossed and i == per - 1
             col_stage(k, i, span, col_recv.at[k], col_targets[:len(near)] if near_only else col_targets)
 
-    def raw_stage():
+    def raw_stage(span):
         for s in range(rows):
             pltpu.make_async_remote_copy(
-                src_ref=xs.at[0, s * per + per - 1, :, spans[0]], dst_ref=raw_in.at[s],
-                send_sem=raw_send.at[0], recv_sem=raw_recv.at[0],
+                src_ref=xs.at[0, s * per + per - 1, :, span], dst_ref=raw_in.at[s, :, span],
+                send_sem=sent_sem, recv_sem=raw_recv.at[0],
                 device_id=(r, mirror), device_id_type=MESH,
             ).start()
 
@@ -178,7 +180,7 @@
         for s in row_peers:
             pltpu.make_async_remote_copy(
                 src_ref=raw_in.at[s], dst_ref=raw_all.at[own_rows(), :],
-                send_sem=raw_send.at[1], recv_sem=raw_recv.at[1],
+                send_sem=sent_sem, recv_sem=raw_recv.at[1],
                 device_id=(s, c), device_id_type=MESH,
             ).start()
         raw_all[own_rows(), :] = raw_in[r]
@@ -189,12 +191,12 @@
         high, low = split(raw_all[...])
         both = product(w[0, :2 * grid_y, grid_x * SUB:], high)
         raw_y[...] = both[:grid_y] + both[grid_y:] + product(w[0, :grid_y, grid_x * SUB:], low)
-        at = pl.ds(pl.multiple_of(mirror * part_z, 128), lanes)
+        at = pl.ds(pl.multiple_of(mirror * part_z, 128), raw)
         for m, s in enumerate(near):
             pltpu.make_async_remote_copy(
                 src_ref=raw_y.at[pl.ds(pl.multiple_of(s * share_y, SUB), share_y), :],
                 dst_ref=zbuf.at[per - 1, :, at],
-                send_sem=raw_send.at[2], recv_sem=raw_near.at[m],
+                send_sem=sent_sem, recv_sem=raw_near.at[m],
                 device_id=(r, s), device_id_type=MESH,
             ).start()
         zbuf[per - 1, :, at] = raw_y[pl.ds(pl.multiple_of(c * share_y, SUB), share_y), :]
@@ -278,10 +280,10 @@
         @pl.when(k == 0)
         def _():
             for m in range(len(near), len(col_peers)):
-                came = zbuf.at[0, :, pl.ds(0, per * part_z - lanes)]
+                came = zbuf.at[0, :, pl.ds(0, per * part_z - raw)]
                 pltpu.make_async_copy(came, came, col_recv.at[0, m]).wait()
             for m in range(len(near)):
-                came = zbuf.at[0, :, pl.ds(0, lanes)]
+                came = zbuf.at[0, :, pl.ds(0, raw)]
                 pltpu.make_async_copy(came, came, raw_near.at[m]).wait()
 
         @pl.when(k > 0)
@@ -311,25 +313,30 @@
             last_wait(q, len(col_peers) - 1)
             z_part(last, across[-1] * part_z + span.start, span.size, multiplied if q == len(ends) - 1 else None)
 
-    for p, span in enumerate(spans):
-        load_v[p].wait()
-        split_parts(span)
+    every = range(len(groups))
+    for p, load in enumerate(load_v):
+        load.wait()
+        n = max(0, p + 1 - len(groups))
+        picked = [p] if p < len(groups) else every
+        split_parts(spans[n], picked)
         if p == 0:
             load_w.wait()
-        x_stage(0, span)
-        if p == 0:
+        x_stage(0, spans[n], picked)
+        if p + 1 < len(groups):
+            continue
+        if n == 0:
             pl.semaphore_wait(barrier, len(row_peers) + len(col_peers))
-        row_stage(0, span, first_recv.at[p])
-        if p == 0:
-            raw_stage()
+        row_stage(0, spans[n], first_recv.at[n])
+        if n < raws:
+            raw_stage(spans[n])
     load_rest.start()
     load_t.start()
-    y_stage(0, spans[0], first_recv.at[0], raw=True)
-    load_rest.wait()
-    x_stage(1, whole)
-    row_stage(1, whole, row_recv.at[1])
-    for p, span in enumerate(spans[1:]):
-        y_stage(0, span, first_recv.at[p + 1])
+    for p, span in enumerate(spans):
+        if p == min(2, len(spans) - 1):
+            load_rest.wait()
+            x_stage(1, whole, every)
+            row_stage(1, whole, row_recv.at[0])
+        y_stage(0, span, first_recv.at[p], crossed=p < raws)
     own_z(0)
     raw_row_stage()
     for load in load_symbols:
@@ -340,17 +347,17 @@
     def loop(k, carry):
         @pl.when(k < chunks)
         def _():
-            x_stage(k, whole)
-            row_stage(k, whole, row_recv.at[k])
+            x_stage(k, whole, every)
+            row_stage(k, whole, row_recv.at[k - 1])
 
         @pl.when(k < chunks)
         def _():
-            y_stage(k - 1, whole, row_recv.at[k - 1])
+            y_stage(k - 1, whole, row_recv.at[k - 2])
             own_z(k - 1)
 
         @pl.when(k == chunks)
         def _():
-            last_y_stage(chunks - 1, row_recv.at[chunks - 1])
+            last_y_stage(chunks - 1, row_recv.at[chunks - 2])
             own_z(chunks - 1)
 
         @pl.when(k == 2)
@@ -369,26 +376,24 @@
     lax.fori_loop(2, chunks + lag - 1, loop, 0)
     last_stages()
 
-    sent = rbuf.at[:, pl.ds(0, grid_y - part_y), :]
-    pltpu.make_async_copy(sent, sent, row_send).wait()
-    pltpu.make_async_copy(raw_in, raw_in, raw_send.at[0]).wait()
-    sent = raw_all.at[pl.ds(0, grid_y - part_y), :]
-    pltpu.make_async_copy(sent, sent, raw_send.at[1]).wait()
+    sent = [
+        rbuf.at[:, pl.ds(0, grid_y - part_y), :],
+        raw_in,
+        raw_all.at[pl.ds(0, grid_y - part_y), :],
+        zbuf.at[pl.ds(1, grid_x // rows - 1), :, pl.ds(0, grid_z - part_z)],
+        zbuf.at[0, :, pl.ds(0, grid_z - part_z - half * raw)],
+    ]
     if near:
-        sent = raw_y.at[pl.ds(0, len(near) * share_y), :]
-        pltpu.make_async_copy(sent, sent, raw_send.at[2]).wait()
-    for sent in (
-        zbuf.at[pl.ds(1, grid_x // rows - 1), :, pl.ds(0, grid_z - part_z)],
-        zbuf.at[0, :, pl.ds(0, grid_z - part_z - half * lanes)],
-    ):
-        pltpu.make_async_copy(sent, sent, col_send).wait()
+        sent.append(raw_y.at[pl.ds(0, len(near) * share_y), :])
+    for ref in sent:
+        pltpu.make_async_copy(ref, ref, sent_sem).wait()
 
 
 def transformed(rows, cols, velocity, symbol_x, symbol_y, symbol_z):
     grid_x, part_y, part_z = velocity.shape
     grid_y, grid_z = part_y * rows, part_z * cols
     share_x, share_y = grid_x // rows, grid_y // cols
-    chunks = min(8, share_x)
+    chunks, raws = min(8, share_x), 1
     per = share_x // chunks
     tile = 256
     hx, hy, hz = fixed_table(grid_x), fixed_table(grid_y), fixed_table(grid_z)
@@ -404,7 +409,7 @@
     hbm = pl.BlockSpec(memory_space=pltpu.HBM)
     vmem = pl.BlockSpec(memory_space=pltpu.VMEM)
     return pl.pallas_call(
-        functools.partial(kernel, (rows, cols, chunks, per, 2, 128)),
+        functools.partial(kernel, (rows, cols, chunks, per, 2, 128, raws)),
         out_shape=jax.ShapeDtypeStruct((share_x, share_y, grid_z), f32),
         in_specs=[hbm] * 6,
         out_specs=vmem,
@@ -419,23 +424,21 @@
             pltpu.VMEM((share_x, share_y, grid_z), f32),
             pltpu.VMEM((2 * per * share_y, grid_z), bf16),
             pltpu.VMEM((per, share_y, grid_z), f32),
-            pltpu.VMEM((rows, part_y, 128), f32),
-            pltpu.VMEM((grid_y, 128), f32),
-            pltpu.VMEM((grid_y, 128), f32),
+            pltpu.VMEM((rows, part_y, raws * 128), f32),
+            pltpu.VMEM((grid_y, raws * 128), f32),
+            pltpu.VMEM((grid_y, raws * 128), f32),
             pltpu.VMEM((1, grid_x), f32),
             pltpu.VMEM((1, grid_y), f32),
             pltpu.VMEM((1, grid_z), f32),
             pltpu.VMEM((grid_x, 128), f32),
             pltpu.VMEM((grid_y, 128), f32),
             pltpu.SemaphoreType.DMA((6,)),
-            pltpu.SemaphoreType.DMA((part_z // 128,)),
+            pltpu.SemaphoreType.DMA((part_z // 128 + part_y // SUB - 1,)),
             pltpu.SemaphoreType.DMA,
-            pltpu.SemaphoreType.DMA((chunks, per)),
+            pltpu.SemaphoreType.DMA((chunks - 1, per)),
             pltpu.SemaphoreType.DMA((part_z // 128, per)),
-            pltpu.SemaphoreType.DMA,
-            pltpu.SemaphoreType.DMA((chunks, cols - 1)),
+            pltpu.SemaphoreType.DMA((chunks - 1, cols - 1)),
             pltpu.SemaphoreType.DMA((3, cols - 1)),
-            pltpu.SemaphoreType.DMA((3,)),
             pltpu.SemaphoreType.DMA((2,)),
             pltpu.SemaphoreType.DMA((max(1, cols // 2 - 1),)),
         ],

time: 102 us -> 101 us (level)
  no operation moved by 1% of the time
where the time goes in v4:
time: 101 us
  Pallas kernels  98.9 us (98%)
  local copies, waits for them, and re-layouts  2.02 us (2%)
    pallas_call x1, Pallas kernels, transformed(): pl.pallas_call(functools.partial(kernel, (rows, cols, chunks, per, 2, 128...  98.9 us

profile of v4, /device:TPU:0, one launch (start us, length us, event | category | flops | bytes accessed | tf_op | source)
XLA Modules:
  0.0 100.9 jit_solution(9195728396704319222)
XLA Ops:
  0.0 98.9 %shard_map.64 = f32[16,32,2048]{2,1,0:T(8,128)S(1)} custom-call(f32[128,16,512]{2,1,0:T(8,128)} %v_hbm.1, bf16[8,256,1152]{2,1,0:T(8,128)(2,1)} %constant.4.clone.w_hbm, bf16[2,8,2048,256]{3,2,1,0:T(8,128)(2,1)} %constant.5.clone.t_hbm, f32[1,128]{1,0:T(1,128)} %bitcast.4, f32[1,128]{1,0:T(1,128)} %bitcast.5, f32[1,2048]{1,0:T(1,128)} %bitcast.3), custom_call_target="tpu_custom_call" | custom-call | tf_op jit(solution)/shard_map/pallas_call | solution.py:411
  98.9 2.0 %copy.8 = f32[16,32,2048]{2,1,0:T(8,128)} copy(f32[16,32,2048]{2,1,0:T(8,128)S(1)} %shard_map.64) | data formatting | bytes 8388608

commit v5 on v4

--- a/solution.py
+++ b/solution.py
@@ -62,8 +62,7 @@
     v, w, t, v_parts, xs, rbuf, ybuf, zbuf, lhs, factors, raw_in, raw_all, raw_y, sx_row, sy_row, sz_ref, sx_col, sy_col,
     load_sem, v_sem, sent_sem, row_recv, first_recv, col_recv, last_recv, raw_recv, raw_near,
 ):
-    rows, cols, chunks, per, lag, lanes, raws = dims
-    raw = raws * lanes
+    rows, cols, chunks, per, lag, lanes = dims
     part_y, part_z = v.shape[1], v.shape[2]
     grid_x, grid_y = v.shape[0], rbuf.shape[1]
     share_y, grid_z = zbuf.shape[1], zbuf.shape[2]
@@ -72,7 +71,8 @@
     spans = [pl.ds(p * lanes, lanes) for p in range(part_z // lanes)]
 
     load_w = pltpu.make_async_copy(w_hbm.at[0], w.at[0], load_sem.at[1])
-    load_rest = pltpu.make_async_copy(w_hbm.at[pl.ds(1, chunks - 1)], w.at[pl.ds(1, chunks - 1)], load_sem.at[2])
+    load_next = pltpu.make_async_copy(w_hbm.at[1], w.at[1], load_sem.at[6])
+    load_rest = pltpu.make_async_copy(w_hbm.at[pl.ds(2, chunks - 2)], w.at[pl.ds(2, chunks - 2)], load_sem.at[2])
     load_t = pltpu.make_async_copy(t_hbm, t, load_sem.at[0])
     groups = [pl.ds(g * SUB, SUB) for g in range(part_y // SUB)]
     parts = [(group, spans[0]) for group in groups] + [(pl.ds(0, part_y), span) for span in spans[1:]]
@@ -94,6 +94,11 @@
     depth = (half - 1 - c) * (1 - side) + (c - half) * side
     marks = list(range(half - 1)) + [2 * half - 2 - depth] * half
     col_targets = list(zip(col_peers, marks))
+    raw_widths = [2 * lanes] + [lanes] * (half - 1)
+
+    def by_depth(body):
+        for d in range(half):
+            pl.when(depth == d)(functools.partial(body, d, raw_widths[d]))
 
     barrier = pltpu.get_barrier_semaphore()
     for s in row_peers:
@@ -101,7 +106,7 @@
     for s in col_peers:
         pl.semaphore_signal(barrier, inc=1, device_id=(r, s), device_id_type=MESH)
     load_w.start()
-    for load in load_v + load_symbols:
+    for load in load_v[:len(groups)]:
         load.start()
 
     step = SUB * SUB
@@ -137,12 +142,13 @@
         for i in range(per):
             for s in row_peers:
                 pltpu.make_async_remote_copy(
-                    src_ref=xs.at[k, s * per + i, :, span],
+                    src_ref=xs.at[k, i * rows + s, :, span],
                     dst_ref=rbuf.at[k * per + i, own_rows(), span],
                     send_sem=sent_sem, recv_sem=recv.at[i],
                     device_id=(s, c), device_id_type=MESH,
                 ).start()
-        rbuf[pl.ds(k * per, per), own_rows(), span] = xs[k, pl.ds(r * per, per), :, span]
+        for i in range(per):
+            rbuf[k * per + i, own_rows(), span] = xs[k, i * rows + r, :, span]
 
     def y_plane(k, i, span, recv):
         came = rbuf.at[k * per + i, pl.ds(0, grid_y - part_y), span]
@@ -161,45 +167,67 @@
                 device_id=(r, s), device_id_type=MESH,
             ).start()
 
-    def y_stage(k, span, recv, crossed=False):
+    def y_stage(k, span, recv):
         for i in range(per):
             y_plane(k, i, span, recv)
-            near_only = crossed and i == per - 1
-            col_stage(k, i, span, col_recv.at[k], col_targets[:len(near)] if near_only else col_targets)
-
-    def raw_stage(span):
-        for s in range(rows):
-            pltpu.make_async_remote_copy(
-                src_ref=xs.at[0, s * per + per - 1, :, span], dst_ref=raw_in.at[s, :, span],
-                send_sem=sent_sem, recv_sem=raw_recv.at[0],
-                device_id=(r, mirror), device_id_type=MESH,
-            ).start()
-
-    def raw_row_stage():
-        pltpu.make_async_copy(raw_in, raw_in, raw_recv.at[0]).wait()
+            col_stage(k, i, span, col_recv.at[k], col_targets[len(near):] + col_targets[:len(near)])
+
+    def first_y_stage(p):
+        span = spans[p]
+        for i in range(per):
+            y_plane(0, i, span, first_recv.at[p])
+
+            def cross(d, width):
+                if i < per - 1 or p * lanes >= width:
+                    col_stage(0, i, span, col_recv.at[0], col_targets[len(near):])
+
+            by_depth(cross)
+            col_stage(0, i, span, col_recv.at[0], col_targets[:len(near)])
+
+    def raw_stage(p):
+        span = spans[p]
+
+        def send(d, width):
+            if p * lanes < width:
+                pltpu.make_async_remote_copy(
+                    src_ref=xs.at[0, pl.ds((per - 1) * rows, rows), :, span], dst_ref=raw_in.at[:, :, span],
+                    send_sem=sent_sem, recv_sem=raw_recv.at[0],
+                    device_id=(r, mirror), device_id_type=MESH,
+                ).start()
+
+        by_depth(send)
+
+    def raw_row_stage(d, width):
+        came = raw_in.at[:, :, pl.ds(0, width)]
+        pltpu.make_async_copy(came, came, raw_recv.at[0]).wait()
         for s in row_peers:
             pltpu.make_async_remote_copy(
-                src_ref=raw_in.at[s], dst_ref=raw_all.at[own_rows(), :],
+                src_ref=raw_in.at[s, :, pl.ds(0, width)], dst_ref=raw_all.at[own_rows(), pl.ds(0, width)],
                 send_sem=sent_sem, recv_sem=raw_recv.at[1],
                 device_id=(s, c), device_id_type=MESH,
             ).start()
-        raw_all[own_rows(), :] = raw_in[r]
-
-    def raw_y_stage():
-        came = raw_all.at[pl.ds(0, grid_y - part_y), :]
+        raw_all[own_rows(), :width] = raw_in[r, :, :width]
+
+    def raw_y_stage(d, width):
+        came = raw_all.at[pl.ds(0, grid_y - part_y), pl.ds(0, width)]
         pltpu.make_async_copy(came, came, raw_recv.at[1]).wait()
-        high, low = split(raw_all[...])
+        high, low = split(raw_all[:, :width])
         both = product(w[0, :2 * grid_y, grid_x * SUB:], high)
-        raw_y[...] = both[:grid_y] + both[grid_y:] + product(w[0, :grid_y, grid_x * SUB:], low)
-        at = pl.ds(pl.multiple_of(mirror * part_z, 128), raw)
+        raw_y[:, :width] = both[:grid_y] + both[grid_y:] + product(w[0, :grid_y, grid_x * SUB:], low)
+        at = pl.ds(pl.multiple_of(mirror * part_z, 128), width)
         for m, s in enumerate(near):
             pltpu.make_async_remote_copy(
-                src_ref=raw_y.at[pl.ds(pl.multiple_of(s * share_y, SUB), share_y), :],
+                src_ref=raw_y.at[pl.ds(pl.multiple_of(s * share_y, SUB), share_y), pl.ds(0, width)],
                 dst_ref=zbuf.at[per - 1, :, at],
                 send_sem=sent_sem, recv_sem=raw_near.at[m],
                 device_id=(r, s), device_id_type=MESH,
             ).start()
-        zbuf[per - 1, :, at] = raw_y[pl.ds(pl.multiple_of(c * share_y, SUB), share_y), :]
+        zbuf[per - 1, :, at] = raw_y[pl.ds(pl.multiple_of(c * share_y, SUB), share_y), :width]
+
+    def raw_waits(d, width):
+        for m in range(len(near)):
+            came = zbuf.at[0, :, pl.ds(0, raw_widths[d ^ (m + 1)])]
+            pltpu.make_async_copy(came, came, raw_near.at[m]).wait()
 
     def last_y_stage(k, recv):
         for i in range(per):
@@ -279,12 +307,10 @@
     def across_stage(k):
         @pl.when(k == 0)
         def _():
-            for m in range(len(near), len(col_peers)):
-                came = zbuf.at[0, :, pl.ds(0, per * part_z - raw)]
-                pltpu.make_async_copy(came, came, col_recv.at[0, m]).wait()
-            for m in range(len(near)):
-                came = zbuf.at[0, :, pl.ds(0, raw)]
-                pltpu.make_async_copy(came, came, raw_near.at[m]).wait()
+            for j in range(half):
+                came = zbuf.at[0, :, pl.ds(0, per * part_z - raw_widths[half - 1 - j])]
+                pltpu.make_async_copy(came, came, col_recv.at[0, len(near) + j]).wait()
+            by_depth(raw_waits)
 
         @pl.when(k > 0)
         def _():
@@ -316,6 +342,11 @@
     every = range(len(groups))
     for p, load in enumerate(load_v):
         load.wait()
+        if p == 0:
+            for later in load_v[len(groups):]:
+                later.start()
+        if p == len(groups):
+            load_next.start()
         n = max(0, p + 1 - len(groups))
         picked = [p] if p < len(groups) else every
         split_parts(spans[n], picked)
@@ -327,20 +358,20 @@
         if n == 0:
             pl.semaphore_wait(barrier, len(row_peers) + len(col_peers))
         row_stage(0, spans[n], first_recv.at[n])
-        if n < raws:
-            raw_stage(spans[n])
-    load_rest.start()
-    load_t.start()
-    for p, span in enumerate(spans):
-        if p == min(2, len(spans) - 1):
-            load_rest.wait()
-            x_stage(1, whole, every)
-            row_stage(1, whole, row_recv.at[0])
-        y_stage(0, span, first_recv.at[p], crossed=p < raws)
+        if n < 2:
+            raw_stage(n)
+    for load in load_symbols + [load_rest, load_t]:
+        load.start()
+    load_next.wait()
+    x_stage(1, whole, every)
+    row_stage(1, whole, row_recv.at[0])
+    for p in range(len(spans)):
+        first_y_stage(p)
     own_z(0)
-    raw_row_stage()
+    by_depth(raw_row_stage)
     for load in load_symbols:
         load.wait()
+    load_rest.wait()
     for ref, column in ((sx_row, sx_col), (sy_row, sy_col)):
         column[...] = jnp.broadcast_to(ref[...], (128, ref.shape[1])).T
 
@@ -362,7 +393,7 @@
 
         @pl.when(k == 2)
         def _():
-            raw_y_stage()
+            by_depth(raw_y_stage)
             load_t.wait()
 
         own_stage(k - lag)
@@ -376,28 +407,31 @@
     lax.fori_loop(2, chunks + lag - 1, loop, 0)
     last_stages()
 
-    sent = [
-        rbuf.at[:, pl.ds(0, grid_y - part_y), :],
-        raw_in,
-        raw_all.at[pl.ds(0, grid_y - part_y), :],
-        zbuf.at[pl.ds(1, grid_x // rows - 1), :, pl.ds(0, grid_z - part_z)],
-        zbuf.at[0, :, pl.ds(0, grid_z - part_z - half * raw)],
-    ]
-    if near:
-        sent.append(raw_y.at[pl.ds(0, len(near) * share_y), :])
-    for ref in sent:
-        pltpu.make_async_copy(ref, ref, sent_sem).wait()
+    def drain(d, width):
+        sent = [
+            rbuf.at[:, pl.ds(0, grid_y - part_y), :],
+            raw_in.at[:, :, pl.ds(0, width)],
+            raw_all.at[pl.ds(0, grid_y - part_y), pl.ds(0, width)],
+            zbuf.at[pl.ds(1, grid_x // rows - 1), :, pl.ds(0, grid_z - part_z)],
+            zbuf.at[0, :, pl.ds(0, grid_z - part_z - half * width)],
+        ]
+        if near:
+            sent.append(raw_y.at[pl.ds(0, len(near) * share_y), pl.ds(0, width)])
+        for ref in sent:
+            pltpu.make_async_copy(ref, ref, sent_sem).wait()
+
+    by_depth(drain)
 
 
 def transformed(rows, cols, velocity, symbol_x, symbol_y, symbol_z):
     grid_x, part_y, part_z = velocity.shape
     grid_y, grid_z = part_y * rows, part_z * cols
     share_x, share_y = grid_x // rows, grid_y // cols
-    chunks, raws = min(8, share_x), 1
+    chunks = min(8, share_x)
     per = share_x // chunks
     tile = 256
     hx, hy, hz = fixed_table(grid_x), fixed_table(grid_y), fixed_table(grid_z)
-    order = np.arange(grid_x).reshape(rows, chunks, per).transpose(1, 0, 2).reshape(chunks, rows * per)
+    order = np.arange(grid_x).reshape(rows, chunks, per).transpose(1, 2, 0).reshape(chunks, rows * per)
     w = np.stack([np.kron(hx[o], np.eye(SUB, dtype=np.float32)) for o in order])
     w = np.concatenate(halves(w), axis=1)
     h = np.concatenate(halves(hy), axis=0)
@@ -409,7 +443,7 @@
     hbm = pl.BlockSpec(memory_space=pltpu.HBM)
     vmem = pl.BlockSpec(memory_space=pltpu.VMEM)
     return pl.pallas_call(
-        functools.partial(kernel, (rows, cols, chunks, per, 2, 128, raws)),
+        functools.partial(kernel, (rows, cols, chunks, per, 2, 128)),
         out_shape=jax.ShapeDtypeStruct((share_x, share_y, grid_z), f32),
         in_specs=[hbm] * 6,
         out_specs=vmem,
@@ -424,15 +458,15 @@
             pltpu.VMEM((share_x, share_y, grid_z), f32),
             pltpu.VMEM((2 * per * share_y, grid_z), bf16),
             pltpu.VMEM((per, share_y, grid_z), f32),
-            pltpu.VMEM((rows, part_y, raws * 128), f32),
-            pltpu.VMEM((grid_y, raws * 128), f32),
-            pltpu.VMEM((grid_y, raws * 128), f32),
+            pltpu.VMEM((rows, part_y, 2 * 128), f32),
+            pltpu.VMEM((grid_y, 2 * 128), f32),
+            pltpu.VMEM((grid_y, 2 * 128), f32),
             pltpu.VMEM((1, grid_x), f32),
             pltpu.VMEM((1, grid_y), f32),
             pltpu.VMEM((1, grid_z), f32),
             pltpu.VMEM((grid_x, 128), f32),
             pltpu.VMEM((grid_y, 128), f32),
-            pltpu.SemaphoreType.DMA((6,)),
+            pltpu.SemaphoreType.DMA((7,)),
             pltpu.SemaphoreType.DMA((part_z // 128 + part_y // SUB - 1,)),
             pltpu.SemaphoreType.DMA,
             pltpu.SemaphoreType.DMA((chunks - 1, per)),
@@ -455,7 +489,7 @@
     held = 7 * grid_x * part_y * part_z * 4 + 4 * grid_z * grid_z + 4 * (grid_x * SUB) ** 2
     even = rows & (rows - 1) == 0 and cols & (cols - 1) == 0 and cols > 1 and grid_x % (16 * rows) == 0
     even = even and grid_x * part_z <= 8 * rows * grid_z
-    return even and part_y % SUB == 0 and part_z % 128 == 0 and (part_y * rows) % (SUB * cols) == 0 and held < 54 * 2**20
+    return even and part_y % SUB == 0 and part_z % 256 == 0 and (part_y * rows) % (SUB * cols) == 0 and held < 54 * 2**20
 
 
 def local(rows, cols, velocity, symbol_x, symbol_y, symbol_z):

time: 101 us -> 101 us (level)
  no operation moved by 1% of the time
where the time goes in v5:
time: 101 us; the launch traced here: 100 us
  Pallas kernels  98 us (97%)
  local copies, waits for them, and re-layouts  2.02 us (2%)
    pallas_call x1, Pallas kernels, transformed(): pl.pallas_call(functools.partial(kernel, (rows, cols, chunks, per, 2, 128...  98 us

profile of v5, /device:TPU:0, one launch (start us, length us, event | category | flops | bytes accessed | tf_op | source)
XLA Modules:
  0.0 100.1 jit_solution(11462713543878809791)
XLA Ops:
  0.0 98.0 %shard_map.64 = f32[16,32,2048]{2,1,0:T(8,128)S(1)} custom-call(f32[128,16,512]{2,1,0:T(8,128)} %v_hbm.1, bf16[8,256,1152]{2,1,0:T(8,128)(2,1)} %constant.4.clone.w_hbm, bf16[2,8,2048,256]{3,2,1,0:T(8,128)(2,1)} %constant.5.clone.t_hbm, f32[1,128]{1,0:T(1,128)} %bitcast.4, f32[1,128]{1,0:T(1,128)} %bitcast.5, f32[1,2048]{1,0:T(1,128)} %bitcast.3), custom_call_target="tpu_custom_call" | custom-call | tf_op jit(solution)/shard_map/pallas_call | solution.py:445
  98.1 2.0 %copy.8 = f32[16,32,2048]{2,1,0:T(8,128)} copy(f32[16,32,2048]{2,1,0:T(8,128)S(1)} %shard_map.64) | data formatting | bytes 8388608

commit v6 on v5

--- a/solution.py
+++ b/solution.py
@@ -71,7 +71,7 @@
     spans = [pl.ds(p * lanes, lanes) for p in range(part_z // lanes)]
 
     load_w = pltpu.make_async_copy(w_hbm.at[0], w.at[0], load_sem.at[1])
-    load_next = pltpu.make_async_copy(w_hbm.at[1], w.at[1], load_sem.at[6])
+    load_next = pltpu.make_async_copy(w_hbm.at[1], w.at[1], load_sem.at[4])
     load_rest = pltpu.make_async_copy(w_hbm.at[pl.ds(2, chunks - 2)], w.at[pl.ds(2, chunks - 2)], load_sem.at[2])
     load_t = pltpu.make_async_copy(t_hbm, t, load_sem.at[0])
     groups = [pl.ds(g * SUB, SUB) for g in range(part_y // SUB)]
@@ -80,8 +80,8 @@
         pltpu.make_async_copy(v_hbm.at[:, y, z], v.at[:, y, z], v_sem.at[p]) for p, (y, z) in enumerate(parts)
     ]
     load_symbols = [
-        pltpu.make_async_copy(source, target, load_sem.at[3 + n])
-        for n, (source, target) in enumerate(((sx_hbm, sx_row), (sy_hbm, sy_row), (sz_hbm, sz_ref)))
+        pltpu.make_async_copy(source, target, load_sem.at[3])
+        for source, target in ((sx_hbm, sx_row), (sy_hbm, sy_row), (sz_hbm, sz_ref))
     ]
     half = cols // 2
     side = c // half
@@ -157,20 +157,25 @@
         both = product(w[0, :2 * grid_y, grid_x * SUB:], high)
         ybuf[k, i, :, span] = both[:grid_y] + both[grid_y:] + product(w[0, :grid_y, grid_x * SUB:], low)
 
+    def col_at(k, mark):
+        if isinstance(mark, int) and mark < len(near):
+            return k * half + mark
+        return k * half + len(near) + (mark - len(near)) * (k // (chunks - 2))
+
     def col_stage(k, i, span, recv, targets):
         at = pl.ds(pl.multiple_of(c * part_z + span.start, 128), span.size)
         for s, mark in targets:
             pltpu.make_async_remote_copy(
                 src_ref=ybuf.at[k, i, pl.ds(pl.multiple_of(s * share_y, SUB), share_y), span],
                 dst_ref=zbuf.at[k * per + i, :, at],
-                send_sem=sent_sem, recv_sem=recv.at[mark],
+                send_sem=sent_sem, recv_sem=col_recv.at[col_at(k, mark)] if recv is None else recv.at[mark],
                 device_id=(r, s), device_id_type=MESH,
             ).start()
 
     def y_stage(k, span, recv):
         for i in range(per):
             y_plane(k, i, span, recv)
-            col_stage(k, i, span, col_recv.at[k], col_targets[len(near):] + col_targets[:len(near)])
+            col_stage(k, i, span, None, col_targets[len(near):] + col_targets[:len(near)])
 
     def first_y_stage(p):
         span = spans[p]
@@ -179,10 +184,10 @@
 
             def cross(d, width):
                 if i < per - 1 or p * lanes >= width:
-                    col_stage(0, i, span, col_recv.at[0], col_targets[len(near):])
+                    col_stage(0, i, span, None, col_targets[len(near):])
 
             by_depth(cross)
-            col_stage(0, i, span, col_recv.at[0], col_targets[:len(near)])
+            col_stage(0, i, span, None, col_targets[:len(near)])
 
     def raw_stage(p):
         span = spans[p]
@@ -244,7 +249,7 @@
 
     def col_wait(k, m):
         came = zbuf.at[pl.ds(k * per, per), :, pl.ds(0, part_z)]
-        pltpu.make_async_copy(came, came, col_recv.at[k, m]).wait()
+        pltpu.make_async_copy(came, came, col_recv.at[col_at(k, m)]).wait()
 
     def factor_parts(k, n):
         y_part = sy_col[pl.ds(pl.multiple_of(c * share_y, SUB), share_y), :]
@@ -307,15 +312,14 @@
     def across_stage(k):
         @pl.when(k == 0)
         def _():
-            for j in range(half):
-                came = zbuf.at[0, :, pl.ds(0, per * part_z - raw_widths[half - 1 - j])]
-                pltpu.make_async_copy(came, came, col_recv.at[0, len(near) + j]).wait()
+            came = zbuf.at[0, :, pl.ds(0, half * per * part_z - sum(raw_widths))]
+            pltpu.make_async_copy(came, came, col_recv.at[len(near)]).wait()
             by_depth(raw_waits)
 
         @pl.when(k > 0)
         def _():
-            for m in range(len(near), len(col_peers)):
-                col_wait(k, m)
+            came = zbuf.at[pl.ds(k * per, per), :, pl.ds(0, half * part_z)]
+            pltpu.make_async_copy(came, came, col_recv.at[col_at(k, len(near))]).wait()
 
         z_part(k, (1 - side) * half * part_z, half * part_z, scaled)
 
@@ -466,12 +470,12 @@
             pltpu.VMEM((1, grid_z), f32),
             pltpu.VMEM((grid_x, 128), f32),
             pltpu.VMEM((grid_y, 128), f32),
-            pltpu.SemaphoreType.DMA((7,)),
+            pltpu.SemaphoreType.DMA((5,)),
             pltpu.SemaphoreType.DMA((part_z // 128 + part_y // SUB - 1,)),
             pltpu.SemaphoreType.DMA,
             pltpu.SemaphoreType.DMA((chunks - 1, per)),
             pltpu.SemaphoreType.DMA((part_z // 128, per)),
-            pltpu.SemaphoreType.DMA((chunks - 1, cols - 1)),
+            pltpu.SemaphoreType.DMA(((chunks - 1) * (cols // 2) + cols // 2 - 1,)),
             pltpu.SemaphoreType.DMA((3, cols - 1)),
             pltpu.SemaphoreType.DMA((2,)),
             pltpu.SemaphoreType.DMA((max(1, cols // 2 - 1),)),
@@ -488,7 +492,7 @@
     grid_z = part_z * cols
     held = 7 * grid_x * part_y * part_z * 4 + 4 * grid_z * grid_z + 4 * (grid_x * SUB) ** 2
     even = rows & (rows - 1) == 0 and cols & (cols - 1) == 0 and cols > 1 and grid_x % (16 * rows) == 0
-    even = even and grid_x * part_z <= 8 * rows * grid_z
+    even = even and grid_x * part_z * (cols // 2) <= 8 * rows * grid_z
     return even and part_y % SUB == 0 and part_z % 256 == 0 and (part_y * rows) % (SUB * cols) == 0 and held < 54 * 2**20
 
 

time: 101 us -> 101 us (level)
  no operation moved by 1% of the time
where the time goes in v6:
time: 101 us; the launch traced here: 100 us
  Pallas kernels  98 us (97%)
  local copies, waits for them, and re-layouts  2.02 us (2%)
    pallas_call x1, Pallas kernels, transformed(): pl.pallas_call(functools.partial(kernel, (rows, cols, chunks, per, 2, 128...  98 us

profile of v6, /device:TPU:0, one launch (start us, length us, event | category | flops | bytes accessed | tf_op | source)
XLA Modules:
  0.0 100.1 jit_solution(15238833671347804772)
XLA Ops:
  0.0 98.0 %shard_map.64 = f32[16,32,2048]{2,1,0:T(8,128)S(1)} custom-call(f32[128,16,512]{2,1,0:T(8,128)} %v_hbm.1, bf16[8,256,1152]{2,1,0:T(8,128)(2,1)} %constant.4.clone.w_hbm, bf16[2,8,2048,256]{3,2,1,0:T(8,128)(2,1)} %constant.5.clone.t_hbm, f32[1,128]{1,0:T(1,128)} %bitcast.4, f32[1,128]{1,0:T(1,128)} %bitcast.5, f32[1,2048]{1,0:T(1,128)} %bitcast.3), custom_call_target="tpu_custom_call" | custom-call | tf_op jit(solution)/shard_map/pallas_call | solution.py:449
  98.0 2.0 %copy.8 = f32[16,32,2048]{2,1,0:T(8,128)} copy(f32[16,32,2048]{2,1,0:T(8,128)S(1)} %shard_map.64) | data formatting | bytes 8388608
